TPU v7x, 32 devices: a whole 2x2x4 slice. The times are simulated.
32 devices in a mesh: ep: 16 (over z, y, x), tp: 2 (over core).
Axes of the slice: x: 2, y: 2, z: 4, core: 2. Of those that a mesh axis runs over, the one named last changes fastest.
Arguments:
- tokens: bfloat16 [512, 6144], P('ep', 'tp'), may hold values from -6 to 6
- expert_ids: int32 [512, 8], P('ep'), may hold values from 0 to 15, all different within a row; in each aligned block of 32 rows (0 to 31, 32 to 63, ...) at most 30 rows name the same one
- gate_scores: float32 [512, 8], P('ep'), may hold values from 0.05 to 0.6
- routed_gate: bfloat16 [16, 6144, 2048], P('ep', None, 'tp'), may hold values from -0.078125 to 0.078125
- routed_up: bfloat16 [16, 6144, 2048], P('ep', None, 'tp'), may hold values from -0.078125 to 0.078125
- routed_down: bfloat16 [16, 2048, 6144], P('ep', 'tp'), may hold values from -0.1875 to 0.1875
- shared_gate: bfloat16 [6144, 2048], P(None, 'tp'), may hold values from -0.078125 to 0.078125
- shared_up: bfloat16 [6144, 2048], P(None, 'tp'), may hold values from -0.078125 to 0.078125
- shared_down: bfloat16 [2048, 6144], P('tp'), may hold values from -0.1875 to 0.1875
Outputs:
- moe_out: bfloat16 [512, 6144], P('ep', 'tp')
Inputs may be any that keep to these rules, and one draw needn't show every extreme that they name: `expert_ids`: each row names 8 different experts. Among the 32 rows of one aligned block no expert is named more than 30 times, and in some block one expert is named exactly 30 times.
All inputs are finite; a program needn't handle non-finite values.
Results may differ from a plain program's by a relative error of at most 0.019.
Values may be sent and summed in bfloat16 or wider, within the bound.
A program may use at most 128 MiB of HBM per device.

v0:
```python
import jax
import jax.numpy as jnp
from jax import lax
from jax.sharding import PartitionSpec as P


def routing(expert_ids, gate_scores, experts, capacity):
    row_count, top_count = expert_ids.shape
    entries = expert_ids.reshape(-1)
    onehot = (entries[:, None] == jnp.arange(experts, dtype=jnp.int32)[None, :]).astype(jnp.int32)
    before = jnp.cumsum(onehot, axis=0, dtype=jnp.int32) - onehot
    slot_rank = jnp.sum(before * onehot, axis=1)
    position = entries * capacity + slot_rank
    places = jnp.arange(experts * capacity, dtype=jnp.int32)[:, None] == position[None, :]
    places = places.reshape(experts * capacity, row_count, top_count).astype(jnp.float32)
    select = jnp.sum(places, axis=2).astype(jnp.bfloat16)
    combine_weights = jnp.sum(places * gate_scores[None, :, :], axis=2)
    return (select, combine_weights)


def fold_maker(w_gate, w_up, block_piece):
    return (
        jnp.dot(block_piece, w_gate, preferred_element_type=jnp.float32),
        jnp.dot(block_piece, w_up, preferred_element_type=jnp.float32),
    )


def bucketed(
    tokens,
    expert_ids,
    gate_scores,
    routed_gate,
    routed_up,
    routed_down,
    shared_gate,
    shared_up,
    shared_down,
):
    experts = routed_gate.shape[0] * lax.axis_size("ep")
    row_count, top_count = expert_ids.shape
    capacity = min(row_count, row_count * top_count * 15 // (8 * experts))
    select, combine_weights = routing(expert_ids, gate_scores, experts, capacity)
    width_local = tokens.shape[1]
    buckets = jnp.dot(select, tokens, preferred_element_type=jnp.float32).astype(jnp.bfloat16)
    buckets = buckets.reshape(experts, capacity, width_local)
    w_gate = routed_gate[0]
    w_up = routed_up[0]
    w_down = routed_down[0]
    shared_gate_sum, shared_up_sum = fold_maker(
        shared_gate, shared_up, lax.all_gather(tokens, "tp", axis=1, tiled=True)
    )
    shared_hidden = (jax.nn.silu(shared_gate_sum) * shared_up_sum).astype(jnp.bfloat16)
    shared_partial = jnp.dot(shared_hidden, shared_down, preferred_element_type=jnp.float32).astype(
        jnp.bfloat16
    )
    shared_out = lax.psum_scatter(shared_partial, "tp", scatter_dimension=1, tiled=True).astype(
        jnp.float32
    )
    received = lax.all_to_all(buckets, "ep", split_axis=0, concat_axis=0, tiled=True)
    gate_sum, up_sum = fold_maker(w_gate, w_up, lax.all_gather(received, "tp", axis=2, tiled=True))
    hidden = (jax.nn.silu(gate_sum) * up_sum).astype(jnp.bfloat16)
    partial_value = jnp.dot(hidden, w_down, preferred_element_type=jnp.float32).astype(jnp.bfloat16)
    summed = (
        lax.psum_scatter(partial_value, "tp", scatter_dimension=2, tiled=True)
        .astype(jnp.float32)
        .astype(jnp.bfloat16)
    )
    returned = lax.all_to_all(summed, "ep", split_axis=0, concat_axis=0, tiled=True)
    flat_returned = returned.reshape(experts * capacity, width_local).astype(jnp.float32)
    routed = jnp.einsum(
        "pt,pd->td", combine_weights, flat_returned, precision=lax.Precision.HIGHEST
    )
    return (routed + shared_out).astype(jnp.bfloat16)


def dense(
    tokens,
    expert_ids,
    gate_scores,
    routed_gate,
    routed_up,
    routed_down,
    shared_gate,
    shared_up,
    shared_down,
):
    ep, tp = (lax.axis_size("ep"), lax.axis_size("tp"))
    me = lax.axis_index("ep")
    rows, width = tokens.shape
    units = shared_gate.shape[1] // ep
    own = jnp.arange(ep, dtype=jnp.int32)
    scores = jnp.sum(
        jnp.where(expert_ids[:, :, None] == own[None, None, :], gate_scores[:, :, None], 0.0),
        axis=1,
    )
    scores = lax.all_gather(scores, "ep", axis=0, tiled=True)
    weight = lax.dynamic_slice_in_dim(scores, me, 1, axis=1)
    held = lax.all_gather(tokens, ("ep", "tp"), axis=0, tiled=False).reshape(ep, tp, rows, width)
    features = [held[:, t].reshape(ep * rows, width) for t in range(tp)]
    s_gate = lax.dynamic_slice_in_dim(shared_gate, me * units, units, axis=1)
    s_up = lax.dynamic_slice_in_dim(shared_up, me * units, units, axis=1)
    s_down = lax.dynamic_slice_in_dim(shared_down, me * units, units, axis=0)

    def project(w):
        return sum(
            (
                jnp.dot(
                    features[t], w[t * width : (t + 1) * width], preferred_element_type=jnp.float32
                )
                for t in range(tp)
            )
        )

    hidden = (jax.nn.silu(project(routed_gate[0])) * project(routed_up[0]) * weight).astype(
        jnp.bfloat16
    )
    s_hidden = (jax.nn.silu(project(s_gate)) * project(s_up)).astype(jnp.bfloat16)
    parts = []
    for t in range(tp):
        cut = slice(t * width, (t + 1) * width)
        part = jnp.dot(hidden, routed_down[0][:, cut], preferred_element_type=jnp.float32)
        part = part + jnp.dot(s_hidden, s_down[:, cut], preferred_element_type=jnp.float32)
        parts.append(part.astype(jnp.bfloat16).reshape(ep, 1, rows, width))
    partial = jnp.concatenate(parts, axis=1).reshape(ep * tp, rows, width)
    return lax.psum_scatter(partial, ("ep", "tp"), scatter_dimension=0, tiled=False)


def solution(mesh):
    placed = (
        P("ep", "tp"),
        P("ep", None),
        P("ep", None),
        P("ep", None, "tp"),
        P("ep", None, "tp"),
        P("ep", "tp", None),
        P(None, "tp"),
        P(None, "tp"),
        P("tp", None),
    )

    def local(*args):
        even = args[6].shape[1] % mesh.shape["ep"] == 0
        return (dense if even else bucketed)(*args)

    return jax.shard_map(
        local, mesh=mesh, in_specs=placed, out_specs=P("ep", "tp"), check_vma=False
    )
```

profile of v0, /device:TPU:0, one launch (start us, length us, event | category | flops | bytes accessed | tf_op | source)
XLA Modules:
  0.0 255.7 jit_solution(11739752585782691501)
XLA Ops:
  6.5 0.7 all-gather.4.cloned.1.call-update
  7.3 0.0 reduce-scatter.2.cloned.1.call-start
  7.3 0.7 select_reduce_fusion
  8.0 43.4 %all-gather.1 = f32[16,32,16]{1,2,0:T(8,128)S(1)} all-gather(f32[1,32,16]{1,2,0:T(8,128)S(1)} %bitcast.58), channel_id=1, replica_groups=mesh['ep'=16,'tp'=2] {'ep'}, dimensions={0}, use_global_device_ids=true | all-gather | bytes 34816 | tf_op jit(solution)/shard_map/all_gather | solution.py:96
  51.5 0.1 reshape.25
  51.6 30.7 %all-gather.4.cloned.1.call-done = bf16[1024,3072]{1,0:T(8,128)(2,1)} async-done(((bf16[32,3072]{1,0:T(8,128)(2,1)}), bf16[1024,3072]{1,0:T(8,128)(2,1)}) %all-gather.4.cloned.1.call-update) | async-done | bytes 6291472 | tf_op jit(solution)/shard_map/all_gather | solution.py:98
  82.3 3.6 %fusion.33 = (bf16[16,1,32,3072]{3,2,1,0:T(8,128)(2,1)S(1)}, bf16[16,1,32,3072]{3,2,1,0:T(8,128)(2,1)S(1)}) fusion(bf16[16,2,32,3072]{3,2,1,0:T(8,128)(2,1)} %bitcast.57), kind=kLoop, calls=%fused_computation.40 | loop fusion | bytes 12582912 | tf_op jit(solution)/shard_map/slice | solution.py:99
  85.9 2.9 %copy-done = bf16[1,6144,1024]{2,1,0:T(8,128)(2,1)S(1)} copy-done((bf16[1,6144,1024]{2,1,0:T(8,128)(2,1)S(1)}, bf16[1,6144,1024]{2,1,0:T(8,128)(2,1)}, u32[]{:S(2)}) %copy-start) | copy-done | bytes 12582936
  88.8 3.4 %fusion.6 = f32[512,1024]{1,0:T(8,128)S(1)} fusion(bf16[512,3072]{1,0:T(8,128)(2,1)S(1)} %bitcast.50, bf16[1,6144,1024]{2,1,0:T(8,128)(2,1)S(1)} %copy-done), kind=kOutput, calls=%fused_computation.7 | convolution fusion | flops 3221225472 | bytes 11534336 | tf_op jit(solution)/shard_map/dot_general | solution.py:107
  92.2 4.7 %fusion.4 = f32[512,1024]{1,0:T(8,128)} fusion(bf16[512,3072]{1,0:T(8,128)(2,1)S(1)} %bitcast.46, bf16[1,6144,1024]{2,1,0:T(8,128)(2,1)S(1)} %copy-done), kind=kOutput, calls=%fused_computation.5 | convolution fusion | flops 3221225472 | bytes 11534336 | tf_op jit(solution)/shard_map/dot_general | solution.py:107
  96.9 3.4 %fusion.8 = f32[512,1024]{1,0:T(8,128)S(1)} fusion(bf16[512,3072]{1,0:T(8,128)(2,1)S(1)} %bitcast.47, bf16[1,6144,1024]{2,1,0:T(8,128)(2,1)S(1)} %bitcast.61), kind=kOutput, calls=%fused_computation.9 | convolution fusion | flops 3221225472 | bytes 11534336 | tf_op jit(solution)/shard_map/dot_general | solution.py:107
  100.4 6.8 %multiply_convert_fusion = bf16[512,1024]{1,0:T(8,128)(2,1)S(1)} fusion(f32[512,1024]{1,0:T(8,128)S(1)} %fusion.6, f32[512,1024]{1,0:T(8,128)S(1)} %copy-done.1, f32[512,1024]{1,0:T(8,128)S(1)} %fusion.8, bf16[512,3072]{1,0:T(8,128)(2,1)S(1)} %bitcast.51, bf16[1,6144,1024]{2,1,0:T(8,128)(2,1)} %param.12, f32[512]{0:T(512)S(1)} %bitcast.59), kind=kOutput, calls=%fused_computation.19 | convolution fusion | flops 3225944064 | bytes 16779264 | tf_op jit(solution)/shard_map/dot_general | solution.py:107
  107.2 5.9 %fusion = f32[512,3072]{1,0:T(8,128)S(1)} fusion(bf16[512,1024]{1,0:T(8,128)(2,1)S(1)} %multiply_convert_fusion, bf16[1024,6144]{1,0:T(8,128)(2,1)} %bitcast.62), kind=kOutput, calls=%fused_computation | convolution fusion | flops 3221225472 | bytes 13631488 | tf_op jit(solution)/shard_map/dot_general | solution.py:121
  113.1 3.4 %fusion.2 = f32[512,3072]{1,0:T(8,128)S(1)} fusion(bf16[512,1024]{1,0:T(8,128)(2,1)S(1)} %multiply_convert_fusion, bf16[1024,6144]{1,0:T(8,128)(2,1)S(1)} %bitcast.65), kind=kOutput, calls=%fused_computation.2 | convolution fusion | flops 3221225472 | bytes 13631488 | tf_op jit(solution)/shard_map/dot_general | solution.py:121
  116.6 2.7 %fusion.23 = f32[64,512]{1,0:T(8,128)S(1)} fusion(bf16[512,3072]{1,0:T(8,128)(2,1)S(1)} %bitcast.52, bf16[6144,1024]{1,0:T(8,128)(2,1)} %param.16, s32[]{:T(128)S(6)} %select_n.14), kind=kOutput, calls=%fused_computation.27 | convolution fusion | flops 201326592 | bytes 4063236 | tf_op jit(solution)/shard_map/dot_general | solution.py:107
  119.3 2.7 %fusion.26 = f32[64,512]{1,0:T(8,128)S(1)} fusion(bf16[512,3072]{1,0:T(8,128)(2,1)S(1)} %bitcast.53, bf16[6144,1024]{1,0:T(8,128)(2,1)} %param.15, s32[]{:T(128)S(6)} %select_n.14), kind=kOutput, calls=%fused_computation.30 | convolution fusion | flops 201326592 | bytes 4063236 | tf_op jit(solution)/shard_map/dot_general | solution.py:107
  122.0 2.7 %fusion.20 = f32[512,64]{0,1:T(8,128)S(1)} fusion(f32[64,512]{1,0:T(8,128)S(1)} %fusion.26, bf16[512,3072]{1,0:T(8,128)(2,1)S(1)} %bitcast.48, bf16[6144,1024]{1,0:T(8,128)(2,1)} %param.15, s32[]{:T(128)S(6)} %add.54, s32[]{:T(128)S(6)} %select_n.14), kind=kOutput, calls=%fused_computation.24 | convolution fusion | flops 201359360 | bytes 4194312 | tf_op jit(solution)/shard_map/dot_general | solution.py:107
  124.7 2.7 %fusion.21 = bf16[512,64]{0,1:T(8,128)(2,1)S(1)} fusion(f32[64,512]{1,0:T(8,128)S(1)} %fusion.23, bf16[512,3072]{1,0:T(8,128)(2,1)S(1)} %bitcast.49, bf16[6144,1024]{1,0:T(8,128)(2,1)} %param.16, s32[]{:T(128)S(6)} %add.54, s32[]{:T(128)S(6)} %select_n.14, f32[512,64]{0,1:T(8,128)S(1)} %fusion.20), kind=kOutput, calls=%fused_computation.25 | convolution fusion | flops 201555968 | bytes 4259848 | tf_op jit(solution)/shard_map/dot_general | solution.py:107
  127.4 2.0 add_convert_fusion
  129.4 2.0 add_convert_fusion.1
  131.4 0.6 pad_maximum_fusion
  132.0 3.2 %copy.24 = bf16[16,2,32,3072]{3,2,1,0:T(8,128)(2,1)} copy(bf16[16,2,32,3072]{3,2,0,1:T(8,128)(2,1)S(1)} %pad_maximum_fusion) | data formatting | bytes 12582912 | tf_op jit(solution)/shard_map/concatenate | solution.py:124
  135.2 0.0 reduce-scatter.2.cloned.1.call-update
  135.2 113.7 %reduce-scatter.2.cloned.1.call-done = bf16[1,32,3072]{2,1,0:T(8,128)(2,1)} async-done(((bf16[32,32,3072]{2,1,0:T(8,128)(2,1)}), bf16[1,32,3072]{2,1,0:T(8,128)(2,1)}) %reduce-scatter.2.cloned.1.call-update) | async-done | bytes 196624 | tf_op jit(solution)/shard_map/reduce_scatter | solution.py:125
  (20 shorter events, 0.1 us)
Async XLA Ops:
  6.5 75.8 %all-gather.4.cloned.1.call-start = ((), (), s32[]{:S(2)}) async-start(), calls=%async_computation.2 | async-start | bytes 6488064 | tf_op jit(solution)/shard_map/all_gather | solution.py:98
  7.3 241.7 %reduce-scatter.2.cloned.1.call-start = ((), (), s32[]{:S(2)}) async-start(), calls=%async_computation.1 | async-start | bytes 6488064 | tf_op jit(solution)/shard_map/reduce_scatter | solution.py:125
  82.3 6.4 %copy-start = (bf16[1,6144,1024]{2,1,0:T(8,128)(2,1)S(1)}, bf16[1,6144,1024]{2,1,0:T(8,128)(2,1)}, u32[]{:S(2)}) copy-start(bf16[1,6144,1024]{2,1,0:T(8,128)(2,1)} %param.13) | copy-start | bytes 37748740
  88.8 8.2 %slice-start = ((s8[12582912]{0:T(1024)(128)(4,1)}), s8[4194304]{0:T(1024)(128)(4,1)S(1)}, s32[]{:S(2)}) async-start(s8[12582912]{0:T(1024)(128)(4,1)} %bitcast.60), calls=%async_computation.3 | async-start | bytes 8388608
  88.8 8.2 %slice-start.1 = ((s8[12582912]{0:T(1024)(128)(4,1)}), s8[4194304]{0:T(1024)(128)(4,1)S(1)}, s32[]{:S(2)}) async-start(s8[12582912]{0:T(1024)(128)(4,1)} %bitcast.60), calls=%async_computation.4 | async-start | bytes 8388608
  92.2 4.8 %slice-start.2 = ((s8[12582912]{0:T(1024)(128)(4,1)}), s8[4194304]{0:T(1024)(128)(4,1)S(1)}, s32[]{:S(2)}) async-start(s8[12582912]{0:T(1024)(128)(4,1)} %bitcast.60), calls=%async_computation.5 | async-start | bytes 8388608
  96.9 3.4 %copy-start.1 = (f32[512,1024]{1,0:T(8,128)S(1)}, f32[512,1024]{1,0:T(8,128)}, u32[]{:S(2)}) copy-start(f32[512,1024]{1,0:T(8,128)} %fusion.4) | copy-start | bytes 6291460
  100.4 12.7 %slice-start.3 = ((s8[12582912]{0:T(1024)(128)(4,1)}), s8[4194304]{0:T(1024)(128)(4,1)S(1)}, s32[]{:S(2)}) async-start(s8[12582912]{0:T(1024)(128)(4,1)} %bitcast.63), calls=%async_computation.6 | async-start | bytes 8388608
  100.4 12.7 %slice-start.4 = ((s8[12582912]{0:T(1024)(128)(4,1)}), s8[4194304]{0:T(1024)(128)(4,1)S(1)}, s32[]{:S(2)}) async-start(s8[12582912]{0:T(1024)(128)(4,1)} %bitcast.63), calls=%async_computation.7 | async-start | bytes 8388608
  107.2 5.9 %slice-start.5 = ((s8[12582912]{0:T(1024)(128)(4,1)}), s8[4194304]{0:T(1024)(128)(4,1)S(1)}, s32[]{:S(2)}) async-start(s8[12582912]{0:T(1024)(128)(4,1)} %bitcast.63), calls=%async_computation.8 | async-start | bytes 8388608
Sparse Core Ops, SparseCore 0:
  10.2 72.0 all-gather.3
  135.3 113.5 reduce-scatter.1
where the time goes:
time: 256 us
  waiting for transfers between devices  145 us (57%)
  blocking collectives  43.4 us (17%)
  matrix products  42.4 us (17%)
  between operations  13.6 us (5%)
  local copies, waits for them, and re-layouts  9.85 us (4%)
    reduce_scatter x1, waiting for transfers between devices, dense(): lax.psum_scatter(partial, ('ep', 'tp'), scatter_dimension=0, tiled=False)  114 us
    all_gather x1, blocking collectives, dense(): scores = lax.all_gather(scores, 'ep', axis=0, tiled=True)  43.4 us
    all_gather x1, waiting for transfers between devices, dense(): lax.all_gather(tokens, ('ep', 'tp'), axis=0, tiled=False)  30.7 us
    dot_general x8, matrix products, project(): jnp.dot(features[t], w[t * width:(t + 1) * width], preferred_element_type...  29.1 us
    dot_general x2, matrix products, dense(): jnp.dot(hidden, routed_down[0][:, cut], preferred_element_type=jnp.float32)  9.29 us
  transfers between devices with their start and end apart: 2, of which 2 were waited for; matrix products, arithmetic and copies ran while one was open for 0% of the time, Pallas kernels for 0%

commit v1 on v0

--- a/solution.py
+++ b/solution.py
@@ -93,7 +93,12 @@
         jnp.where(expert_ids[:, :, None] == own[None, None, :], gate_scores[:, :, None], 0.0),
         axis=1,
     )
-    scores = lax.all_gather(scores, "ep", axis=0, tiled=True)
+    ring = [scores]
+    for hop in range(15):
+        ring.append(lax.ppermute(ring[-1], "ep", [(dev, (dev + 1) % 16) for dev in range(16)]))
+    scores = jnp.roll(
+        jnp.concatenate(ring[::-1], axis=0), (lax.axis_index("ep") + 1) * ring[0].shape[0], axis=0
+    )
     weight = lax.dynamic_slice_in_dim(scores, me, 1, axis=1)
     held = lax.all_gather(tokens, ("ep", "tp"), axis=0, tiled=False).reshape(ep, tp, rows, width)
     features = [held[:, t].reshape(ep * rows, width) for t in range(tp)]

time: 256 us -> 290 us (1.13)
  waiting for transfers between devices: 145 us -> 220 us
  blocking collectives: 43.4 us -> 0 us
  starting transfers between devices: 0.04 us -> 3.1 us
    ppermute x0 -> x15, waiting for transfers between devices: none -> 108 us  [dense(): lax.ppermute(ring[-1], 'ep', [(dev, (dev + 1) % 16) for dev in range(16)])]
    all_gather x1 -> x0, blocking collectives: 43.4 us -> none  [dense(): scores = lax.all_gather(scores, 'ep', axis=0, tiled=True)]
    all_gather x1, waiting for transfers between devices: 30.7 us -> 0.01 us  [dense(): lax.all_gather(tokens, ('ep', 'tp'), axis=0, tiled=False)]
    ppermute x0 -> x15, starting transfers between devices: none -> 3.06 us  [dense(): lax.ppermute(ring[-1], 'ep', [(dev, (dev + 1) % 16) for dev in range(16)])]
  transfers between devices with their start and end apart: 2 -> 17, of which waited for: 2 -> 16; matrix products, arithmetic and copies ran while one was open for 0% -> 0% of each run, Pallas kernels for 0% -> 0%
where the time goes in v1:
time: 290 us
  waiting for transfers between devices  220 us (76%)
  matrix products  42.4 us (15%)
  between operations  13.6 us (5%)
  local copies, waits for them, and re-layouts  9.87 us (3%)
  starting transfers between devices  3.1 us (1%)
    reduce_scatter x1, waiting for transfers between devices, dense(): lax.psum_scatter(partial, ('ep', 'tp'), scatter_dimension=0, tiled=False)  111 us
    ppermute x15, waiting for transfers between devices, dense(): lax.ppermute(ring[-1], 'ep', [(dev, (dev + 1) % 16) for dev in range(16)])  108 us
    dot_general x8, matrix products, project(): jnp.dot(features[t], w[t * width:(t + 1) * width], preferred_element_type...  29.1 us
    dot_general x2, matrix products, dense(): jnp.dot(hidden, routed_down[0][:, cut], preferred_element_type=jnp.float32)  9.29 us
  transfers between devices with their start and end apart: 17, of which 16 were waited for; matrix products, arithmetic and copies ran while one was open for 0% of the time, Pallas kernels for 0%

profile of v1, /device:TPU:0, one launch (start us, length us, event | category | flops | bytes accessed | tf_op | source)
XLA Modules:
  0.0 289.9 jit_solution(9143285464296544743)
XLA Ops:
  11.0 5.6 %collective-permute-done = f32[32,16]{0,1:T(8,128)S(1)} collective-permute-done((f32[32,16]{0,1:T(8,128)S(1)}, f32[32,16]{0,1:T(8,128)S(1)}, u32[]{:S(2)}, u32[]{:S(2)}) %collective-permute-start) | collective-permute-done | bytes 2080 | tf_op jit(solution)/shard_map/ppermute | solution.py:98
  16.7 7.2 %collective-permute-done.1 = f32[32,16]{0,1:T(8,128)S(1)} collective-permute-done((f32[32,16]{0,1:T(8,128)S(1)}, f32[32,16]{0,1:T(8,128)S(1)}, u32[]{:S(2)}, u32[]{:S(2)}) %collective-permute-start.1) | collective-permute-done | bytes 2080 | tf_op jit(solution)/shard_map/ppermute | solution.py:98
  23.9 7.4 %collective-permute-done.2 = f32[32,16]{0,1:T(8,128)S(1)} collective-permute-done((f32[32,16]{0,1:T(8,128)S(1)}, f32[32,16]{0,1:T(8,128)S(1)}, u32[]{:S(2)}, u32[]{:S(2)}) %collective-permute-start.2) | collective-permute-done | bytes 2080 | tf_op jit(solution)/shard_map/ppermute | solution.py:98
  31.3 7.2 %collective-permute-done.3 = f32[32,16]{0,1:T(8,128)S(1)} collective-permute-done((f32[32,16]{0,1:T(8,128)S(1)}, f32[32,16]{0,1:T(8,128)S(1)}, u32[]{:S(2)}, u32[]{:S(2)}) %collective-permute-start.3) | collective-permute-done | bytes 2080 | tf_op jit(solution)/shard_map/ppermute | solution.py:98
  38.5 7.4 %collective-permute-done.4 = f32[32,16]{0,1:T(8,128)S(1)} collective-permute-done((f32[32,16]{0,1:T(8,128)S(1)}, f32[32,16]{0,1:T(8,128)S(1)}, u32[]{:S(2)}, u32[]{:S(2)}) %collective-permute-start.4) | collective-permute-done | bytes 2080 | tf_op jit(solution)/shard_map/ppermute | solution.py:98
  45.9 7.3 %collective-permute-done.5 = f32[32,16]{0,1:T(8,128)S(1)} collective-permute-done((f32[32,16]{0,1:T(8,128)S(1)}, f32[32,16]{0,1:T(8,128)S(1)}, u32[]{:S(2)}, u32[]{:S(2)}) %collective-permute-start.5) | collective-permute-done | bytes 2080 | tf_op jit(solution)/shard_map/ppermute | solution.py:98
  53.2 7.2 %collective-permute-done.6 = f32[32,16]{0,1:T(8,128)S(1)} collective-permute-done((f32[32,16]{0,1:T(8,128)S(1)}, f32[32,16]{0,1:T(8,128)S(1)}, u32[]{:S(2)}, u32[]{:S(2)}) %collective-permute-start.6) | collective-permute-done | bytes 2080 | tf_op jit(solution)/shard_map/ppermute | solution.py:98
  60.4 7.6 %collective-permute-done.7 = f32[32,16]{0,1:T(8,128)S(1)} collective-permute-done((f32[32,16]{0,1:T(8,128)S(1)}, f32[32,16]{0,1:T(8,128)S(1)}, u32[]{:S(2)}, u32[]{:S(2)}) %collective-permute-start.7) | collective-permute-done | bytes 2080 | tf_op jit(solution)/shard_map/ppermute | solution.py:98
  68.0 7.3 %collective-permute-done.8 = f32[32,16]{0,1:T(8,128)S(1)} collective-permute-done((f32[32,16]{0,1:T(8,128)S(1)}, f32[32,16]{0,1:T(8,128)S(1)}, u32[]{:S(2)}, u32[]{:S(2)}) %collective-permute-start.8) | collective-permute-done | bytes 2080 | tf_op jit(solution)/shard_map/ppermute | solution.py:98
  75.3 7.4 %collective-permute-done.9 = f32[32,16]{0,1:T(8,128)S(1)} collective-permute-done((f32[32,16]{0,1:T(8,128)S(1)}, f32[32,16]{0,1:T(8,128)S(1)}, u32[]{:S(2)}, u32[]{:S(2)}) %collective-permute-start.9) | collective-permute-done | bytes 2080 | tf_op jit(solution)/shard_map/ppermute | solution.py:98
  82.7 7.3 %collective-permute-done.10 = f32[32,16]{0,1:T(8,128)S(1)} collective-permute-done((f32[32,16]{0,1:T(8,128)S(1)}, f32[32,16]{0,1:T(8,128)S(1)}, u32[]{:S(2)}, u32[]{:S(2)}) %collective-permute-start.10) | collective-permute-done | bytes 2080 | tf_op jit(solution)/shard_map/ppermute | solution.py:98
  90.0 7.2 %collective-permute-done.11 = f32[32,16]{0,1:T(8,128)S(1)} collective-permute-done((f32[32,16]{0,1:T(8,128)S(1)}, f32[32,16]{0,1:T(8,128)S(1)}, u32[]{:S(2)}, u32[]{:S(2)}) %collective-permute-start.11) | collective-permute-done | bytes 2080 | tf_op jit(solution)/shard_map/ppermute | solution.py:98
  97.3 7.2 %collective-permute-done.12 = f32[32,16]{0,1:T(8,128)S(1)} collective-permute-done((f32[32,16]{0,1:T(8,128)S(1)}, f32[32,16]{0,1:T(8,128)S(1)}, u32[]{:S(2)}, u32[]{:S(2)}) %collective-permute-start.12) | collective-permute-done | bytes 2080 | tf_op jit(solution)/shard_map/ppermute | solution.py:98
  104.5 7.2 %collective-permute-done.13 = f32[32,16]{0,1:T(8,128)S(1)} collective-permute-done((f32[32,16]{0,1:T(8,128)S(1)}, f32[32,16]{0,1:T(8,128)S(1)}, u32[]{:S(2)}, u32[]{:S(2)}) %collective-permute-start.13) | collective-permute-done | bytes 2080 | tf_op jit(solution)/shard_map/ppermute | solution.py:98
  111.8 7.2 %collective-permute-done.14 = f32[32,16]{0,1:T(8,128)S(1)} collective-permute-done((f32[32,16]{0,1:T(8,128)S(1)}, f32[32,16]{0,1:T(8,128)S(1)}, u32[]{:S(2)}, u32[]{:S(2)}) %collective-permute-start.14) | collective-permute-done | bytes 2080 | tf_op jit(solution)/shard_map/ppermute | solution.py:98
  119.2 3.6 %fusion.31 = (bf16[16,1,32,3072]{3,2,1,0:T(8,128)(2,1)S(1)}, bf16[16,1,32,3072]{3,2,1,0:T(8,128)(2,1)S(1)}) fusion(bf16[16,2,32,3072]{3,2,1,0:T(8,128)(2,1)} %bitcast.54), kind=kLoop, calls=%fused_computation.39 | loop fusion | bytes 12582912 | tf_op jit(solution)/shard_map/slice | solution.py:104
  125.7 3.4 %fusion.10 = f32[512,1024]{1,0:T(8,128)S(1)} fusion(bf16[512,3072]{1,0:T(8,128)(2,1)S(1)} %bitcast.47, bf16[1,6144,1024]{2,1,0:T(8,128)(2,1)S(1)} %copy-done), kind=kOutput, calls=%fused_computation.11 | convolution fusion | flops 3221225472 | bytes 11534336 | tf_op jit(solution)/shard_map/dot_general | solution.py:112
  129.1 4.8 %fusion.8 = f32[512,1024]{1,0:T(8,128)} fusion(bf16[512,3072]{1,0:T(8,128)(2,1)S(1)} %bitcast.43, bf16[1,6144,1024]{2,1,0:T(8,128)(2,1)S(1)} %copy-done), kind=kOutput, calls=%fused_computation.9 | convolution fusion | flops 3221225472 | bytes 11534336 | tf_op jit(solution)/shard_map/dot_general | solution.py:112
  133.9 3.4 %fusion.4 = f32[512,1024]{1,0:T(8,128)S(1)} fusion(bf16[512,3072]{1,0:T(8,128)(2,1)S(1)} %bitcast.44, bf16[1,6144,1024]{2,1,0:T(8,128)(2,1)S(1)} %bitcast.57), kind=kOutput, calls=%fused_computation.5 | convolution fusion | flops 3221225472 | bytes 11534336 | tf_op jit(solution)/shard_map/dot_general | solution.py:112
  137.3 6.7 %multiply_convert_fusion = bf16[512,1024]{1,0:T(8,128)(2,1)S(1)} fusion(f32[512,1024]{1,0:T(8,128)S(1)} %fusion.4, f32[512,1024]{1,0:T(8,128)S(1)} %fusion.10, f32[512,1024]{1,0:T(8,128)S(1)} %copy-done.1, f32[512]{0:T(512)S(1)} %bitcast.55, bf16[512,3072]{1,0:T(8,128)(2,1)S(1)} %bitcast.48, bf16[1,6144,1024]{2,1,0:T(8,128)(2,1)} %param.13), kind=kOutput, calls=%fused_computation.19 | convolution fusion | flops 3225944064 | bytes 16779264 | tf_op jit(solution)/shard_map/dot_general | solution.py:112
  144.1 5.9 %fusion = f32[512,3072]{1,0:T(8,128)S(1)} fusion(bf16[512,1024]{1,0:T(8,128)(2,1)S(1)} %multiply_convert_fusion, bf16[1024,6144]{1,0:T(8,128)(2,1)} %bitcast.58), kind=kOutput, calls=%fused_computation | convolution fusion | flops 3221225472 | bytes 13631488 | tf_op jit(solution)/shard_map/dot_general | solution.py:126
  150.0 3.4 %fusion.2 = f32[512,3072]{1,0:T(8,128)S(1)} fusion(bf16[512,1024]{1,0:T(8,128)(2,1)S(1)} %multiply_convert_fusion, bf16[1024,6144]{1,0:T(8,128)(2,1)S(1)} %bitcast.61), kind=kOutput, calls=%fused_computation.2 | convolution fusion | flops 3221225472 | bytes 13631488 | tf_op jit(solution)/shard_map/dot_general | solution.py:126
  168.8 3.2 %copy.16 = bf16[16,2,32,3072]{3,2,1,0:T(8,128)(2,1)} copy(bf16[16,2,32,3072]{3,2,0,1:T(8,128)(2,1)S(1)} %pad_maximum_fusion) | data formatting | bytes 12582912 | tf_op jit(solution)/shard_map/concatenate | solution.py:129
  172.0 111.0 %reduce-scatter.2.cloned.1.call-done = bf16[1,32,3072]{2,1,0:T(8,128)(2,1)} async-done(((bf16[32,32,3072]{2,1,0:T(8,128)(2,1)}), bf16[1,32,3072]{2,1,0:T(8,128)(2,1)}) %reduce-scatter.2.cloned.1.call-update) | async-done | bytes 196624 | tf_op jit(solution)/shard_map/reduce_scatter | solution.py:130
  (48 shorter events, 23.0 us)
Async XLA Ops:
  6.5 112.7 %all-gather.3.cloned.1.call-start = ((), (), s32[]{:S(2)}) async-start(), calls=%async_computation.2 | async-start | bytes 6488064 | tf_op jit(solution)/shard_map/all_gather | solution.py:103
  7.3 275.8 %reduce-scatter.2.cloned.1.call-start = ((), (), s32[]{:S(2)}) async-start(), calls=%async_computation.1 | async-start | bytes 6488064 | tf_op jit(solution)/shard_map/reduce_scatter | solution.py:130
  8.0 8.6 %collective-permute-start = (f32[32,16]{0,1:T(8,128)S(1)}, f32[32,16]{0,1:T(8,128)S(1)}, u32[]{:S(2)}, u32[]{:S(2)}) collective-permute-start(f32[32,16]{0,1:T(8,128)S(1)} %select_reduce_fusion), channel_id=1, source_target_pairs={{0,2},{2,4},{4,6},{6,8},{8,10},{10,12},{12,14},{14,16},{16,18},{18... | collective-permute-start | bytes 6152 | tf_op jit(solution)/shard_map/ppermute | solution.py:98
  16.7 7.2 %collective-permute-start.1 = (f32[32,16]{0,1:T(8,128)S(1)}, f32[32,16]{0,1:T(8,128)S(1)}, u32[]{:S(2)}, u32[]{:S(2)}) collective-permute-start(f32[32,16]{0,1:T(8,128)S(1)} %collective-permute-done), channel_id=1, source_target_pairs={{0,2},{2,4},{4,6},{6,8},{8,10},{10,12},{12,14},{14,16},{16,18},{18... | collective-permute-start | bytes 6152 | tf_op jit(solution)/shard_map/ppermute | solution.py:98
  23.9 7.4 %collective-permute-start.2 = (f32[32,16]{0,1:T(8,128)S(1)}, f32[32,16]{0,1:T(8,128)S(1)}, u32[]{:S(2)}, u32[]{:S(2)}) collective-permute-start(f32[32,16]{0,1:T(8,128)S(1)} %collective-permute-done.1), channel_id=1, source_target_pairs={{0,2},{2,4},{4,6},{6,8},{8,10},{10,12},{12,14},{14,16},{16,18},{18... | collective-permute-start | bytes 6152 | tf_op jit(solution)/shard_map/ppermute | solution.py:98
  31.3 7.2 %collective-permute-start.3 = (f32[32,16]{0,1:T(8,128)S(1)}, f32[32,16]{0,1:T(8,128)S(1)}, u32[]{:S(2)}, u32[]{:S(2)}) collective-permute-start(f32[32,16]{0,1:T(8,128)S(1)} %collective-permute-done.2), channel_id=1, source_target_pairs={{0,2},{2,4},{4,6},{6,8},{8,10},{10,12},{12,14},{14,16},{16,18},{18... | collective-permute-start | bytes 6152 | tf_op jit(solution)/shard_map/ppermute | solution.py:98
  38.5 7.4 %collective-permute-start.4 = (f32[32,16]{0,1:T(8,128)S(1)}, f32[32,16]{0,1:T(8,128)S(1)}, u32[]{:S(2)}, u32[]{:S(2)}) collective-permute-start(f32[32,16]{0,1:T(8,128)S(1)} %collective-permute-done.3), channel_id=1, source_target_pairs={{0,2},{2,4},{4,6},{6,8},{8,10},{10,12},{12,14},{14,16},{16,18},{18... | collective-permute-start | bytes 6152 | tf_op jit(solution)/shard_map/ppermute | solution.py:98
  45.9 7.3 %collective-permute-start.5 = (f32[32,16]{0,1:T(8,128)S(1)}, f32[32,16]{0,1:T(8,128)S(1)}, u32[]{:S(2)}, u32[]{:S(2)}) collective-permute-start(f32[32,16]{0,1:T(8,128)S(1)} %collective-permute-done.4), channel_id=1, source_target_pairs={{0,2},{2,4},{4,6},{6,8},{8,10},{10,12},{12,14},{14,16},{16,18},{18... | collective-permute-start | bytes 6152 | tf_op jit(solution)/shard_map/ppermute | solution.py:98
  53.2 7.2 %collective-permute-start.6 = (f32[32,16]{0,1:T(8,128)S(1)}, f32[32,16]{0,1:T(8,128)S(1)}, u32[]{:S(2)}, u32[]{:S(2)}) collective-permute-start(f32[32,16]{0,1:T(8,128)S(1)} %collective-permute-done.5), channel_id=1, source_target_pairs={{0,2},{2,4},{4,6},{6,8},{8,10},{10,12},{12,14},{14,16},{16,18},{18... | collective-permute-start | bytes 6152 | tf_op jit(solution)/shard_map/ppermute | solution.py:98
  60.4 7.6 %collective-permute-start.7 = (f32[32,16]{0,1:T(8,128)S(1)}, f32[32,16]{0,1:T(8,128)S(1)}, u32[]{:S(2)}, u32[]{:S(2)}) collective-permute-start(f32[32,16]{0,1:T(8,128)S(1)} %collective-permute-done.6), channel_id=1, source_target_pairs={{0,2},{2,4},{4,6},{6,8},{8,10},{10,12},{12,14},{14,16},{16,18},{18... | collective-permute-start | bytes 6152 | tf_op jit(solution)/shard_map/ppermute | solution.py:98
  68.0 7.3 %collective-permute-start.8 = (f32[32,16]{0,1:T(8,128)S(1)}, f32[32,16]{0,1:T(8,128)S(1)}, u32[]{:S(2)}, u32[]{:S(2)}) collective-permute-start(f32[32,16]{0,1:T(8,128)S(1)} %collective-permute-done.7), channel_id=1, source_target_pairs={{0,2},{2,4},{4,6},{6,8},{8,10},{10,12},{12,14},{14,16},{16,18},{18... | collective-permute-start | bytes 6152 | tf_op jit(solution)/shard_map/ppermute | solution.py:98
  75.3 7.4 %collective-permute-start.9 = (f32[32,16]{0,1:T(8,128)S(1)}, f32[32,16]{0,1:T(8,128)S(1)}, u32[]{:S(2)}, u32[]{:S(2)}) collective-permute-start(f32[32,16]{0,1:T(8,128)S(1)} %collective-permute-done.8), channel_id=1, source_target_pairs={{0,2},{2,4},{4,6},{6,8},{8,10},{10,12},{12,14},{14,16},{16,18},{18... | collective-permute-start | bytes 6152 | tf_op jit(solution)/shard_map/ppermute | solution.py:98
  82.7 7.3 %collective-permute-start.10 = (f32[32,16]{0,1:T(8,128)S(1)}, f32[32,16]{0,1:T(8,128)S(1)}, u32[]{:S(2)}, u32[]{:S(2)}) collective-permute-start(f32[32,16]{0,1:T(8,128)S(1)} %collective-permute-done.9), channel_id=1, source_target_pairs={{0,2},{2,4},{4,6},{6,8},{8,10},{10,12},{12,14},{14,16},{16,18},{18... | collective-permute-start | bytes 6152 | tf_op jit(solution)/shard_map/ppermute | solution.py:98
  90.0 7.2 %collective-permute-start.11 = (f32[32,16]{0,1:T(8,128)S(1)}, f32[32,16]{0,1:T(8,128)S(1)}, u32[]{:S(2)}, u32[]{:S(2)}) collective-permute-start(f32[32,16]{0,1:T(8,128)S(1)} %collective-permute-done.10), channel_id=1, source_target_pairs={{0,2},{2,4},{4,6},{6,8},{8,10},{10,12},{12,14},{14,16},{16,18},{18... | collective-permute-start | bytes 6152 | tf_op jit(solution)/shard_map/ppermute | solution.py:98
  97.3 7.2 %collective-permute-start.12 = (f32[32,16]{0,1:T(8,128)S(1)}, f32[32,16]{0,1:T(8,128)S(1)}, u32[]{:S(2)}, u32[]{:S(2)}) collective-permute-start(f32[32,16]{0,1:T(8,128)S(1)} %collective-permute-done.11), channel_id=1, source_target_pairs={{0,2},{2,4},{4,6},{6,8},{8,10},{10,12},{12,14},{14,16},{16,18},{18... | collective-permute-start | bytes 6152 | tf_op jit(solution)/shard_map/ppermute | solution.py:98
  104.5 7.2 %collective-permute-start.13 = (f32[32,16]{0,1:T(8,128)S(1)}, f32[32,16]{0,1:T(8,128)S(1)}, u32[]{:S(2)}, u32[]{:S(2)}) collective-permute-start(f32[32,16]{0,1:T(8,128)S(1)} %collective-permute-done.12), channel_id=1, source_target_pairs={{0,2},{2,4},{4,6},{6,8},{8,10},{10,12},{12,14},{14,16},{16,18},{18... | collective-permute-start | bytes 6152 | tf_op jit(solution)/shard_map/ppermute | solution.py:98
  111.8 7.2 %collective-permute-start.14 = (f32[32,16]{0,1:T(8,128)S(1)}, f32[32,16]{0,1:T(8,128)S(1)}, u32[]{:S(2)}, u32[]{:S(2)}) collective-permute-start(f32[32,16]{0,1:T(8,128)S(1)} %collective-permute-done.13), channel_id=1, source_target_pairs={{0,2},{2,4},{4,6},{6,8},{8,10},{10,12},{12,14},{14,16},{16,18},{18... | collective-permute-start | bytes 6152 | tf_op jit(solution)/shard_map/ppermute | solution.py:98
  119.2 6.4 %copy-start = (bf16[1,6144,1024]{2,1,0:T(8,128)(2,1)S(1)}, bf16[1,6144,1024]{2,1,0:T(8,128)(2,1)}, u32[]{:S(2)}) copy-start(bf16[1,6144,1024]{2,1,0:T(8,128)(2,1)} %param.12) | copy-start | bytes 37748740
  125.7 8.2 %slice-start = ((s8[12582912]{0:T(1024)(128)(4,1)}), s8[4194304]{0:T(1024)(128)(4,1)S(1)}, s32[]{:S(2)}) async-start(s8[12582912]{0:T(1024)(128)(4,1)} %bitcast.56), calls=%async_computation.3 | async-start | bytes 8388608
  125.7 8.2 %slice-start.1 = ((s8[12582912]{0:T(1024)(128)(4,1)}), s8[4194304]{0:T(1024)(128)(4,1)S(1)}, s32[]{:S(2)}) async-start(s8[12582912]{0:T(1024)(128)(4,1)} %bitcast.56), calls=%async_computation.4 | async-start | bytes 8388608
  129.1 4.8 %slice-start.2 = ((s8[12582912]{0:T(1024)(128)(4,1)}), s8[4194304]{0:T(1024)(128)(4,1)S(1)}, s32[]{:S(2)}) async-start(s8[12582912]{0:T(1024)(128)(4,1)} %bitcast.56), calls=%async_computation.5 | async-start | bytes 8388608
  137.3 12.6 %slice-start.3 = ((s8[12582912]{0:T(1024)(128)(4,1)}), s8[4194304]{0:T(1024)(128)(4,1)S(1)}, s32[]{:S(2)}) async-start(s8[12582912]{0:T(1024)(128)(4,1)} %bitcast.59), calls=%async_computation.6 | async-start | bytes 8388608
  137.3 12.6 %slice-start.4 = ((s8[12582912]{0:T(1024)(128)(4,1)}), s8[4194304]{0:T(1024)(128)(4,1)S(1)}, s32[]{:S(2)}) async-start(s8[12582912]{0:T(1024)(128)(4,1)} %bitcast.59), calls=%async_computation.7 | async-start | bytes 8388608
  144.0 5.9 %slice-start.5 = ((s8[12582912]{0:T(1024)(128)(4,1)}), s8[4194304]{0:T(1024)(128)(4,1)S(1)}, s32[]{:S(2)}) async-start(s8[12582912]{0:T(1024)(128)(4,1)} %bitcast.59), calls=%async_computation.8 | async-start | bytes 8388608
  (1 other events, 3.4 us)
Sparse Core Ops, SparseCore 0:
  10.2 72.4 all-gather.2
  172.1 110.8 reduce-scatter.1
